TPU v7x, 32 devices: a 4x2x2 block of a 4x4x8 slice. The times are simulated.
32 devices in a mesh: prob: 4 (over y, z), feat: 8 (over x, core).
Axes of the slice: x: 4, y: 2, z: 2, core: 2. Of those that a mesh axis runs over, the one named last changes fastest.
The devices are a block of a 4x4x8 slice.
Arguments:
- design: bfloat16 [16384, 4096], P(None, ('prob', 'feat')), parts along dimension 1
- w_init: float32 [4096, 8], P(('prob', 'feat')), parts along dimension 0
- targets: float32 [65536, 8], P('prob'), parts along dimension 0
Outputs:
- output 1: float32 [4096, 8], P(('prob', 'feat')), parts along dimension 0
- output 2: float32 [65536, 8], P('prob'), parts along dimension 0
There are 4 independent parts. A program takes and returns all parts, laid end to end along the dimension named above; each array names one.
All inputs are finite; a program needn't handle non-finite values.
Results may differ from a plain program's by a relative error of at most 0.00410973.
Values are sent between devices in bfloat16 or wider.
A program may use at most 768 MiB of HBM per device.

v0:
```python
import jax
import jax.numpy as jnp
from jax import lax
from jax.sharding import PartitionSpec as P

LOCAL_STEPS = 2
SWEEPS = 6
RIDGE = 0.01
GAMMA = 0.75


def block_product(x_block, coef_block):
    full = jnp.dot(x_block, coef_block.astype(jnp.bfloat16), preferred_element_type=jnp.float32)
    return full.astype(jnp.bfloat16).astype(jnp.float32)


def left_product(x_block, resid_part):
    return lax.dot_general(x_block, resid_part.astype(jnp.bfloat16), (((0,), (0,)), ((), ())), preferred_element_type=jnp.float32)


def solution(mesh):
    group_size = mesh.shape['feat']

    def per_device(design, w_init, targets):
        samples = design.shape[0]
        step_size = samples / (group_size * jnp.sum(jnp.square(design.astype(jnp.float32))))
        prediction = lax.psum(block_product(design, w_init), 'feat')
        residual = targets - prediction
        weights = w_init
        for sweep_idx in range(SWEEPS):
            gradient = left_product(design, residual) / samples
            coef_step = step_size * (gradient - RIDGE * weights)
            update = block_product(design, coef_step)
            for step_idx in range(1, LOCAL_STEPS):
                gradient = left_product(design, residual - group_size * update) / samples
                coef_step = coef_step + step_size * (gradient - RIDGE * (weights + coef_step))
                update = block_product(design, coef_step)
            residual = residual - GAMMA * lax.psum(update, 'feat')
            weights = weights + GAMMA * coef_step
        return weights, residual

    return jax.shard_map(
        per_device,
        mesh=mesh,
        in_specs=(P(None, ('prob', 'feat')), P(('prob', 'feat'), None), P('prob', None)),
        out_specs=(P(('prob', 'feat'), None), P('prob', None)),
        check_vma=False,
    )
```

profile of v0, /device:TPU:81, one launch (start us, length us, event | category | flops | bytes accessed | tf_op | source)
XLA Modules:
  0.0 479.1 jit_solution(9174499016199366209)
XLA Ops:
  7.2 0.0 copy-start.3
  7.2 0.1 all-reduce.8.cloned.1.call-start
  7.3 4.2 fusion.42
  11.5 0.0 copy-start.4
  11.5 0.1 all-reduce.8.cloned.1.call-update
  11.5 0.1 all-reduce.10.cloned.1.call-start
  11.6 4.4 multiply_reduce_fusion
  16.7 51.7 %all-reduce.8.cloned.1.call-done = f32[16384,8]{0,1:T(8,128)} async-done(((f32[16384,8]{0,1:T(8,128)}), f32[16384,8]{0,1:T(8,128)}) %all-reduce.8.cloned.1.call-update) | async-done | bytes 524304 | tf_op jit(solution)/shard_map/psum | solution.py:27
  68.4 0.0 copy-done.3
  68.4 1.1 sub.75
  69.5 0.0 copy-done.4
  69.5 2.8 fusion.96
  72.3 5.2 %fusion.78 = f32[128,8]{0,1:T(8,128)S(1)} fusion(f32[128,8]{0,1:T(8,128)S(1)} %fusion.96, bf16[16384,128]{1,0:T(8,128)(2,1)} %param.3, f32[16384,8]{0,1:T(8,128)S(1)} %sub.75, f32[128,8]{0,1:T(8,128)S(1)} %copy-done.4, f32[]{:T(128)S(6)} %div.63), kind=kOutput, calls=%fused_computation.92 | convolution fusion | flops 67771392 | bytes 4730884 | tf_op jit(solution)/shard_map/dot_general | solution.py:18
  77.5 4.2 fusion.36
  81.7 0.1 all-reduce.10.cloned.1.call-update
  81.8 0.1 all-reduce.12.cloned.1.call-start
  81.9 53.8 %all-reduce.10.cloned.1.call-done = f32[16384,8]{0,1:T(8,128)} async-done(((f32[16384,8]{0,1:T(8,128)}), f32[16384,8]{0,1:T(8,128)}) %all-reduce.10.cloned.1.call-update) | async-done | bytes 524304 | tf_op jit(solution)/shard_map/psum | solution.py:38
  135.7 0.0 copy-start.1
  135.7 3.0 fusion.93
  138.8 0.0 copy-done.1
  138.8 5.2 %multiply_add_fusion.4 = (f32[128,8]{0,1:T(8,128)S(1)}, bf16[128,8]{0,1:T(8,128)(2,1)S(1)}) fusion(f32[128,8]{0,1:T(8,128)S(1)} %copy-done.4, f32[128,8]{0,1:T(8,128)S(1)} %fusion.78, f32[128,8]{0,1:T(8,128)S(1)} %fusion.93, bf16[16384,128]{1,0:T(8,128)(2,1)} %param.3, f32[16384,8]{0,1:T(8,128)S(1)} %sub.75, f32[16384,8]{0,1:T(8,128)S(1)} %copy-done.1, ...), kind=kOutput, calls=%fused_computation.139 | convolution fusion | flops 68038656 | bytes 5261316 | tf_op jit(solution)/shard_map/dot_general | solution.py:18
  144.0 4.2 fusion.29
  148.2 0.1 all-reduce.12.cloned.1.call-update
  148.2 0.1 all-reduce.14.cloned.1.call-start
  148.3 53.9 %all-reduce.12.cloned.1.call-done = f32[16384,8]{0,1:T(8,128)} async-done(((f32[16384,8]{0,1:T(8,128)}), f32[16384,8]{0,1:T(8,128)}) %all-reduce.12.cloned.1.call-update) | async-done | bytes 524304 | tf_op jit(solution)/shard_map/psum | solution.py:38
  202.2 1.1 multiply_subtract_fusion.4
  203.3 2.8 fusion.90
  206.1 5.2 %fusion.68 = f32[128,8]{0,1:T(8,128)S(1)} fusion(f32[128,8]{0,1:T(8,128)S(1)} %fusion.90, bf16[16384,128]{1,0:T(8,128)(2,1)} %param.3, f32[16384,8]{0,1:T(8,128)S(1)} %multiply_subtract_fusion.4, f32[128,8]{0,1:T(8,128)S(1)} %get-tuple-element.2, f32[]{:T(128)S(6)} %div.63), kind=kOutput, calls=%fused_computation.82 | convolution fusion | flops 67771392 | bytes 4730884 | tf_op jit(solution)/shard_map/dot_general | solution.py:18
  211.3 4.2 fusion.22
  215.5 0.1 all-reduce.14.cloned.1.call-update
  215.6 0.1 all-reduce.16.cloned.1.call-start
  215.6 53.9 %all-reduce.14.cloned.1.call-done = f32[16384,8]{0,1:T(8,128)} async-done(((f32[16384,8]{0,1:T(8,128)}), f32[16384,8]{0,1:T(8,128)}) %all-reduce.14.cloned.1.call-update) | async-done | bytes 524304 | tf_op jit(solution)/shard_map/psum | solution.py:38
  269.5 0.0 copy-start
  269.5 3.0 fusion.87
  272.5 0.0 copy-done
  272.6 5.2 %multiply_add_fusion.2 = (f32[128,8]{0,1:T(8,128)S(1)}, bf16[128,8]{0,1:T(8,128)(2,1)S(1)}) fusion(f32[128,8]{0,1:T(8,128)S(1)} %get-tuple-element.2, f32[128,8]{0,1:T(8,128)S(1)} %fusion.68, f32[128,8]{0,1:T(8,128)S(1)} %fusion.87, bf16[16384,128]{1,0:T(8,128)(2,1)} %param.3, f32[16384,8]{0,1:T(8,128)S(1)} %multiply_subtract_fusion.4, ...), kind=kOutput, calls=%fused_computation.137 | convolution fusion | flops 68038656 | bytes 5261316 | tf_op jit(solution)/shard_map/dot_general | solution.py:18
  277.8 4.2 fusion.15
  281.9 0.1 all-reduce.16.cloned.1.call-update
  282.0 0.2 all-reduce.18.cloned.1.call-start
  282.3 53.7 %all-reduce.16.cloned.1.call-done = f32[16384,8]{0,1:T(8,128)} async-done(((f32[16384,8]{0,1:T(8,128)}), f32[16384,8]{0,1:T(8,128)}) %all-reduce.16.cloned.1.call-update) | async-done | bytes 524304 | tf_op jit(solution)/shard_map/psum | solution.py:38
  335.9 1.1 multiply_subtract_fusion.2
  337.0 2.8 fusion.84
  339.9 5.2 %fusion.58 = f32[128,8]{0,1:T(8,128)S(1)} fusion(f32[128,8]{0,1:T(8,128)S(1)} %fusion.84, bf16[16384,128]{1,0:T(8,128)(2,1)} %param.3, f32[16384,8]{0,1:T(8,128)S(1)} %multiply_subtract_fusion.2, f32[128,8]{0,1:T(8,128)S(1)} %get-tuple-element.4, f32[]{:T(128)S(6)} %div.63), kind=kOutput, calls=%fused_computation.72 | convolution fusion | flops 67771392 | bytes 4730884 | tf_op jit(solution)/shard_map/dot_general | solution.py:18
  345.1 4.2 fusion.8
  349.3 0.1 all-reduce.18.cloned.1.call-update
  349.3 0.1 all-reduce.20.cloned.1.call-start
  349.4 53.9 %all-reduce.18.cloned.1.call-done = f32[16384,8]{0,1:T(8,128)} async-done(((f32[16384,8]{0,1:T(8,128)}), f32[16384,8]{0,1:T(8,128)}) %all-reduce.18.cloned.1.call-update) | async-done | bytes 524304 | tf_op jit(solution)/shard_map/psum | solution.py:38
  403.3 0.0 copy-start.2
  403.3 3.0 fusion.81
  406.3 0.0 copy-done.2
  406.3 5.8 %multiply_add_fusion = (f32[128,8]{0,1:T(8,128)}, bf16[128,8]{0,1:T(8,128)(2,1)S(1)}) fusion(f32[128,8]{0,1:T(8,128)S(1)} %get-tuple-element.4, f32[128,8]{0,1:T(8,128)S(1)} %fusion.58, f32[128,8]{0,1:T(8,128)S(1)} %fusion.81, bf16[16384,128]{1,0:T(8,128)(2,1)} %param.3, f32[16384,8]{0,1:T(8,128)S(1)} %multiply_subtract_fusion.2, ...), kind=kOutput, calls=%fused_computation.135 | convolution fusion | flops 68038656 | bytes 5261316 | tf_op jit(solution)/shard_map/dot_general | solution.py:18
  412.1 4.2 fusion.1
  416.3 0.1 all-reduce.20.cloned.1.call-update
  416.4 53.9 %all-reduce.20.cloned.1.call-done = f32[16384,8]{0,1:T(8,128)} async-done(((f32[16384,8]{0,1:T(8,128)}), f32[16384,8]{0,1:T(8,128)}) %all-reduce.20.cloned.1.call-update) | async-done | bytes 524304 | tf_op jit(solution)/shard_map/psum | solution.py:38
  470.3 1.9 multiply_subtract_fusion
Async XLA Ops:
  7.2 61.2 %copy-start.3 = (f32[16384,8]{0,1:T(8,128)S(1)}, f32[16384,8]{0,1:T(8,128)}, u32[]{:S(2)}) copy-start(f32[16384,8]{0,1:T(8,128)} %param.5) | copy-start | bytes 1572868
  7.2 61.2 %all-reduce.8.cloned.1.call-start = ((), (), s32[]{:S(2)}) async-start(), calls=%async_computation | async-start | bytes 1048576 | tf_op jit(solution)/shard_map/psum | solution.py:27
  11.5 58.0 %copy-start.4 = (f32[128,8]{0,1:T(8,128)S(1)}, f32[128,8]{0,1:T(8,128)}, u32[]{:S(2)}) copy-start(f32[128,8]{0,1:T(8,128)} %param.4) | copy-start | bytes 12292
  11.5 124.2 %all-reduce.10.cloned.1.call-start = ((), (), s32[]{:S(2)}) async-start(), calls=%async_computation.1 | async-start | bytes 1048576 | tf_op jit(solution)/shard_map/psum | solution.py:38
  81.8 120.4 %all-reduce.12.cloned.1.call-start = ((), (), s32[]{:S(2)}) async-start(), calls=%async_computation.2 | async-start | bytes 1048576 | tf_op jit(solution)/shard_map/psum | solution.py:38
  135.7 3.1 copy-start.1
  148.2 121.3 %all-reduce.14.cloned.1.call-start = ((), (), s32[]{:S(2)}) async-start(), calls=%async_computation.3 | async-start | bytes 1048576 | tf_op jit(solution)/shard_map/psum | solution.py:38
  215.6 120.4 %all-reduce.16.cloned.1.call-start = ((), (), s32[]{:S(2)}) async-start(), calls=%async_computation.4 | async-start | bytes 1048576 | tf_op jit(solution)/shard_map/psum | solution.py:38
  269.5 3.1 copy-start
  282.0 121.3 %all-reduce.18.cloned.1.call-start = ((), (), s32[]{:S(2)}) async-start(), calls=%async_computation.5 | async-start | bytes 1048576 | tf_op jit(solution)/shard_map/psum | solution.py:38
  349.3 121.0 %all-reduce.20.cloned.1.call-start = ((), (), s32[]{:S(2)}) async-start(), calls=%async_computation.6 | async-start | bytes 1048576 | tf_op jit(solution)/shard_map/psum | solution.py:38
  403.3 3.1 copy-start.2
Sparse Core Ops, SparseCore 0:
  11.7 56.6 all-reduce.7
  81.9 53.7 all-reduce.9
  148.3 53.7 all-reduce.11
  215.7 53.7 all-reduce.13
  282.1 53.7 all-reduce.15
  349.5 53.7 all-reduce.17
  416.5 53.7 all-reduce.19
where the time goes:
time: 481 us; the launch traced here: 479 us
  waiting for transfers between devices  375 us (78%)
  matrix products  78.8 us (16%)
  between operations  14.9 us (3%)
  other arithmetic  9.59 us (2%)
    psum x6, waiting for transfers between devices, per_device(): residual = residual - GAMMA * lax.psum(update, 'feat')  323 us
    psum x1, waiting for transfers between devices, per_device(): prediction = lax.psum(block_product(design, w_init), 'feat')  51.7 us
    dot_general x12, matrix products, left_product(): lax.dot_general(x_block, resid_part.astype(jnp.bfloat16), (((0,), (0,)),...  49.5 us
    dot_general x7, matrix products, block_product(): jnp.dot(x_block, coef_block.astype(jnp.bfloat16), preferred_element_type=...  29.3 us
  transfers between devices with their start and end apart: 7, of which 7 were waited for; matrix products, arithmetic and copies ran while one was open for 1% of the time, Pallas kernels for 0%

commit v1 on v0

v1 whole, which is shorter than its diff:
```python
import functools

import jax
import jax.numpy as jnp
from jax import lax
from jax.experimental import pallas as pl
from jax.experimental.pallas import tpu as pltpu
from jax.sharding import PartitionSpec as P

LOCAL_STEPS = 2
SWEEPS = 6
RIDGE = 0.01
GAMMA = 0.75

LANES = 512
MESH = pl.DeviceIdType.MESH


def kernel(group, chunks, x_hbm, w_ref, y_ref, w_out, r_out,
           x, xt, res, upd, inbox,
           x_sem, y_sem, o_sem, rs_send, rs_recv, ag_send, ag_recv, fw_send):
    chips = group // 2
    width = LANES
    blocks = group * chunks
    samples = x.shape[0]
    me = lax.axis_index("feat")
    chip, core = me // 2, me % 2

    def peer(rel):
        return ((chip + rel // 2) % chips) * 2 + (core + rel % 2) % 2

    def back(rel):
        return ((chips - rel // 2) % chips) * 2 + rel % 2

    near = [2 * d for d in range(1, chips)]
    near.sort(key=lambda rel: min(rel // 2, chips - rel // 2))
    far_first = near[::-1]
    sends = [rel + k for rel in far_first for k in (0, 1)] + [1]
    direct = [1] + near

    def x_copy(b):
        rows = pl.ds(b * 2 * width, 2 * width)
        return pltpu.make_async_copy(x_hbm.at[rows], x.at[rows], x_sem.at[b])

    def y_copy(c, h):
        cols = pl.ds(pl.multiple_of(((me * chunks + c) * 2 + h) * width, width), width)
        return pltpu.make_async_copy(y_ref.at[:, cols], res.at[me * chunks + c, pl.ds(8 * h, 8)], y_sem.at[c * 2 + h])

    def rs_copy(rel, c):
        return pltpu.make_async_remote_copy(
            src_ref=upd.at[peer(rel) * chunks + c], dst_ref=inbox.at[c, back(rel)],
            send_sem=rs_send.at[rel, c], recv_sem=rs_recv.at[back(rel), c],
            device_id={"feat": peer(rel)}, device_id_type=MESH)

    def rs_arrival(rel, c):
        return pltpu.make_async_remote_copy(
            src_ref=upd.at[peer(rel) * chunks + c], dst_ref=inbox.at[c, rel],
            send_sem=rs_send.at[rel, c], recv_sem=rs_recv.at[rel, c],
            device_id={"feat": peer(rel)}, device_id_type=MESH)

    def ag_copy(rel, c):
        own = res.at[me * chunks + c]
        return pltpu.make_async_remote_copy(
            src_ref=own, dst_ref=own, send_sem=ag_send.at[rel, c], recv_sem=ag_recv.at[back(rel), c],
            device_id={"feat": peer(rel)}, device_id_type=MESH)

    def fw_copy(rel, c):
        block = res.at[peer(rel) * chunks + c]
        return pltpu.make_async_remote_copy(
            src_ref=block, dst_ref=block, send_sem=fw_send.at[rel // 2, c], recv_sem=ag_recv.at[rel + 1, c],
            device_id={"feat": peer(1)}, device_id_type=MESH)

    def ag_arrival(rel, c):
        block = res.at[peer(rel) * chunks + c]
        return pltpu.make_async_remote_copy(
            src_ref=block, dst_ref=block, send_sem=ag_send.at[rel, c], recv_sem=ag_recv.at[rel, c],
            device_id={"feat": peer(rel)}, device_id_type=MESH)

    def x_pair(b):
        start = pl.multiple_of(b * (2 * width), 2 * width)
        return x[pl.ds(start, width)], x[pl.ds(start + width, width)]

    def two_by_two(coef):
        zero = jnp.zeros_like(coef)
        top = jnp.concatenate([coef, zero], axis=1)
        low = jnp.concatenate([zero, coef], axis=1)
        return jnp.concatenate([top, low], axis=0).astype(jnp.bfloat16)

    def block_product(lhs, b):
        return jnp.dot(lhs, xt[b], preferred_element_type=jnp.float32).astype(jnp.bfloat16)

    def gradient_term(resid, b):
        first, second = x_pair(b)
        return jnp.dot(resid.astype(jnp.bfloat16), jnp.concatenate([first, second], axis=1),
                       preferred_element_type=jnp.float32)

    def gradient_of(acc):
        half = acc.shape[1] // 2
        return (acc[:8, :half] + acc[8:, half:]) * (1.0 / samples)

    def scatter(product):
        pending = None
        for rel in sends:
            for c in range(chunks):
                b = peer(rel) * chunks + c
                upd[b] = product(b)
                if pending is not None:
                    rs_copy(*pending).start()
                pending = (rel, c)
        for c in range(chunks):
            inbox[c, 0] = product(me * chunks + c)
            if pending is not None:
                rs_copy(*pending).start()
                pending = None

    def sum_and_gather(scale):
        for c in range(chunks):
            total = inbox[c, 0].astype(jnp.float32)
            for rel in sends[::-1]:
                rs_arrival(rel, c).wait_recv()
                total = total + inbox[c, rel].astype(jnp.float32)
            b = me * chunks + c
            res[b] = res[b] - scale * total
            for rel in far_first + [1]:
                ag_copy(rel, c).start()

    def gather_arrivals(use):
        late = []
        for c in range(chunks):
            for rel in direct:
                ag_arrival(rel, c).wait_recv()
                if rel != 1:
                    fw_copy(rel, c).start()
                use(rel, c)
            for rel, k in late:
                ag_arrival(rel, k).wait_recv()
                use(rel, k)
            late = [(rel + 1, c) for rel in near]
        for rel, k in late:
            ag_arrival(rel, k).wait_recv()
            use(rel, k)

    def wait_sends():
        for c in range(chunks):
            for rel in sends:
                rs_copy(rel, c).wait_send()
            for rel in direct:
                ag_copy(rel, c).wait_send()
            for rel in near:
                fw_copy(rel, c).wait_send()

    for b in range(blocks):
        x_copy(b).start()
    for c in range(chunks):
        for h in (0, 1):
            y_copy(c, h).start()

    barrier = pltpu.get_barrier_semaphore()
    for rel in range(1, group):
        pl.semaphore_signal(barrier, inc=1, device_id={"feat": peer(rel)}, device_id_type=MESH)
    pl.semaphore_wait(barrier, group - 1)

    for b in range(blocks):
        x_copy(b).wait()
    weights = w_ref[...]
    start_lhs = two_by_two(weights)

    def first_product(b):
        first, second = x_pair(b)
        rows = jnp.concatenate([first, second], axis=1)
        full = lax.dot_general(start_lhs, rows, (((1,), (1,)), ((), ())), preferred_element_type=jnp.float32)
        return full.astype(jnp.bfloat16)

    scatter(first_product)

    def prepare(b, total):
        first, second = x_pair(b)
        half = first.shape[1]
        xt[b, :half] = first.T
        xt[b, half:] = second.T
        both = first.astype(jnp.float32), second.astype(jnp.float32)
        for part in both:
            square = part * part
            total = total + jnp.sum(square.reshape(width // 8, 8, half), axis=0)
        return total

    squares = lax.fori_loop(0, blocks, prepare, jnp.zeros((8, x.shape[1]), jnp.float32))
    step_size = samples / (group * jnp.sum(squares))

    for c in range(chunks):
        for h in (0, 1):
            y_copy(c, h).wait()
    sum_and_gather(1.0)

    def sweep(sweep_idx, weights):
        acc = [jnp.zeros((16, 2 * x.shape[1]), jnp.float32)]
        for c in range(chunks):
            b = me * chunks + c
            acc[0] = acc[0] + gradient_term(res[b], b)

        def use(rel, c):
            b = peer(rel) * chunks + c
            acc[0] = acc[0] + gradient_term(res[b], b)

        gather_arrivals(use)
        coef = step_size * (gradient_of(acc[0]) - RIDGE * weights)
        for step_idx in range(1, LOCAL_STEPS):
            lhs = two_by_two(coef)
            total = jnp.zeros((16, 2 * x.shape[1]), jnp.float32)
            for b in range(blocks):
                product = block_product(lhs, b).astype(jnp.float32)
                total = total + gradient_term(res[b] - group * product, b)
            coef = coef + step_size * (gradient_of(total) - RIDGE * (weights + coef))
        lhs = two_by_two(coef)
        wait_sends()
        scatter(lambda b: block_product(lhs, b))
        sum_and_gather(GAMMA)
        return weights + GAMMA * coef

    w_out[...] = lax.fori_loop(0, SWEEPS, sweep, weights)

    def out_copy(rel, c, h):
        b = peer(rel) * chunks + c
        cols = pl.ds(pl.multiple_of((b * 2 + h) * width, width), width)
        return pltpu.make_async_copy(res.at[b, pl.ds(8 * h, 8)], r_out.at[:, cols], o_sem.at[rel, c * 2 + h])

    def put(rel, c):
        for h in (0, 1):
            out_copy(rel, c, h).start()

    for c in range(chunks):
        put(0, c)
    gather_arrivals(put)
    wait_sends()
    for rel in range(group):
        for c in range(chunks):
            for h in (0, 1):
                out_copy(rel, c, h).wait()


def solution(mesh):
    group = mesh.shape["feat"]

    def per_device(design, w_init, targets):
        samples, feats = design.shape
        outs = targets.shape[1]
        chunks = samples // (2 * LANES * group)
        blocks = group * chunks
        any_space = pl.BlockSpec(memory_space=pl.ANY)
        vmem = pl.BlockSpec(memory_space=pltpu.VMEM)
        weights, residual = pl.pallas_call(
            functools.partial(kernel, group, chunks),
            out_shape=(jax.ShapeDtypeStruct((outs, feats), jnp.float32),
                       jax.ShapeDtypeStruct((outs, samples), jnp.float32)),
            in_specs=[any_space, vmem, any_space],
            out_specs=(vmem, any_space),
            scratch_shapes=[
                pltpu.VMEM((samples, feats), jnp.bfloat16),
                pltpu.VMEM((blocks, 2 * feats, LANES), jnp.bfloat16),
                pltpu.VMEM((blocks, 2 * outs, LANES), jnp.float32),
                pltpu.VMEM((blocks, 2 * outs, LANES), jnp.bfloat16),
                pltpu.VMEM((chunks, group, 2 * outs, LANES), jnp.bfloat16),
                pltpu.SemaphoreType.DMA((blocks,)),
                pltpu.SemaphoreType.DMA((2 * chunks,)),
                pltpu.SemaphoreType.DMA((group, 2 * chunks)),
                pltpu.SemaphoreType.DMA((group, chunks)),
                pltpu.SemaphoreType.DMA((group, chunks)),
                pltpu.SemaphoreType.DMA((group, chunks)),
                pltpu.SemaphoreType.DMA((group, chunks)),
                pltpu.SemaphoreType.DMA((group // 2, chunks)),
            ],
            compiler_params=pltpu.CompilerParams(collective_id=0, has_side_effects=True,
                                                 vmem_limit_bytes=48 * 1024 * 1024),
        )(design, w_init.T, targets.T)
        return weights.T, residual.T

    return jax.shard_map(
        per_device,
        mesh=mesh,
        in_specs=(P(None, ("prob", "feat")), P(("prob", "feat"), None), P("prob", None)),
        out_specs=(P(("prob", "feat"), None), P("prob", None)),
        check_vma=False,
    )
```

time: 481 us -> 109 us (0.23)
  waiting for transfers between devices: 375 us -> 0 us
  Pallas kernels: 0 us -> 103 us
  matrix products: 78.8 us -> 0 us
  between operations: 14.9 us -> 0.65 us
  other arithmetic: 9.59 us -> 0 us
  local copies, waits for them, and re-layouts: 0.03 us -> 5.3 us
    psum x7 -> x0, waiting for transfers between devices: 375 us -> none  [the longest x6 323 us: per_device(): residual = residual - GAMMA * lax.psum(update, 'feat')]
    pallas_call x0 -> x1, Pallas kernels: none -> 103 us  [per_device(): pl.pallas_call(functools.partial(kernel, group, chunks), out_shape=(jax.S...]
    dot_general x19 -> x0, matrix products: 78.8 us -> none  [the longest x12 49.5 us: left_product(): lax.dot_general(x_block, resid_part.astype(jnp.bfloat16), (((0,), (0,)),...]
    unnamed x10 -> x8, local copies, waits for them, and re-layouts: 0.03 us -> 5.3 us
    sub x4 -> x0, other arithmetic: 5.22 us -> none  [the longest x3 4.13 us: per_device(): residual = residual - GAMMA * lax.psum(update, 'feat')]
  transfers between devices with their start and end apart: 7 -> 0, of which waited for: 7 -> 0; matrix products, arithmetic and copies ran while one was open for 1% -> 0% of each run, Pallas kernels for 0% -> 0%
where the time goes in v1:
time: 109 us
  Pallas kernels  103 us (94%)
  local copies, waits for them, and re-layouts  5.3 us (5%)
    pallas_call x1, Pallas kernels, per_device(): pl.pallas_call(functools.partial(kernel, group, chunks), out_shape=(jax.S...  103 us
    unnamed x8, local copies, waits for them, and re-layouts  5.3 us

profile of v1, /device:TPU:81, one launch (start us, length us, event | category | flops | bytes accessed | tf_op | source)
XLA Modules:
  0.0 108.6 jit_solution(160499683808885082)
XLA Ops:
  0.6 0.0 copy-start
  0.6 2.2 %copy-done = bf16[16384,128]{1,0:T(8,128)(2,1)S(1)} copy-done((bf16[16384,128]{1,0:T(8,128)(2,1)S(1)}, bf16[16384,128]{1,0:T(8,128)(2,1)}, u32[]{:S(2)}) %copy-start) | copy-done | bytes 4194328
  2.8 0.0 copy-start.1
  2.8 1.0 copy-done.1
  3.9 0.0 copy-start.2
  3.9 0.7 copy-done.2
  4.5 102.7 %shard_map.50 = (f32[8,128]{1,0:T(8,128)S(1)}, f32[8,16384]{1,0:T(8,128)S(1)}) custom-call(bf16[16384,128]{1,0:T(8,128)(2,1)S(1)} %copy-done, f32[8,128]{1,0:T(8,128)S(1)} %bitcast.7, f32[8,16384]{1,0:T(8,128)S(1)} %bitcast.5), custom_call_target="tpu_custom_call" | custom-call | tf_op jit(solution)/shard_map/pallas_call | solution.py:251
  107.2 0.6 copy.7
  107.8 0.8 copy.8
Async XLA Ops:
  0.6 2.2 %copy-start = (bf16[16384,128]{1,0:T(8,128)(2,1)S(1)}, bf16[16384,128]{1,0:T(8,128)(2,1)}, u32[]{:S(2)}) copy-start(bf16[16384,128]{1,0:T(8,128)(2,1)} %x_hbm.1) | copy-start | bytes 12582916
  2.8 1.0 copy-start.1
  3.9 0.7 copy-start.2

commit v2 on v0

v2 whole, which is shorter than its diff:
```python
import functools

import jax
import jax.numpy as jnp
from jax import lax
from jax.experimental import pallas as pl
from jax.experimental.pallas import tpu as pltpu
from jax.sharding import PartitionSpec as P

LOCAL_STEPS = 2
SWEEPS = 6
RIDGE = 0.01
GAMMA = 0.75

LANES = 512
CHUNKS = (1, 1, 1, 1)
AHEAD = 1
MESH = pl.DeviceIdType.MESH


def kernel(group, per_owner, x_hbm, w_hbm, y_hbm, w_out, r_out,
           x, xt, w_in, res, upd, inbox,
           x_sem, w_sem, y_sem, rs_send, rs_recv, ag_send, ag_recv, fw_send):
    chips = group // 2
    width = LANES
    blocks = chips * per_owner
    samples, feats = x.shape
    me = lax.axis_index("feat")
    chip, core = me // 2, me % 2

    others = sorted(range(1, chips), key=lambda d: -min(d, chips - d))
    everyone = others + [0]
    chunks = []
    for count in CHUNKS:
        chunks.append((sum(n for _, n in chunks), count))
    assert sum(CHUNKS) == per_owner

    def owner(d):
        return (chip + d) % chips

    def on_owner(body):
        pl.when(core == 1)(body)

    def on_helper(body):
        pl.when(core == 0)(body)

    def span(d, c):
        start, count = chunks[c]
        return pl.ds(owner(d) * per_owner + start, count)

    def blocks_of(d, c):
        start, count = chunks[c]
        return [owner(d) * per_owner + start + k for k in range(count)]

    def x_copy(d, c):
        start, count = chunks[c]
        rows = pl.ds(pl.multiple_of((owner(d) * per_owner + start) * 2 * width, 2 * width), count * 2 * width)
        return pltpu.make_async_copy(x_hbm.at[rows], x.at[rows], x_sem.at[d, c])

    def y_copy(k, h):
        b = chip * per_owner + k
        cols = pl.ds(pl.multiple_of((b * 2 + h) * width, width), width)
        return pltpu.make_async_copy(y_hbm.at[:, cols], res.at[b, pl.ds(8 * h, 8)], y_sem.at[k * 2 + h])

    def remote(src, dst, send, recv, chip_to, core_to):
        return pltpu.make_async_remote_copy(src_ref=src, dst_ref=dst, send_sem=send, recv_sem=recv,
                                            device_id={"feat": chip_to * 2 + core_to}, device_id_type=MESH)

    def rs_copy(d, c):
        slot = (chips - d) % chips * 2 + core
        start, count = chunks[c]
        return remote(upd.at[span(d, c)], inbox.at[slot, pl.ds(start, count)],
                      rs_send.at[d, c], rs_recv.at[slot, c], owner(d), 1)

    def rs_arrival(slot, c):
        start, count = chunks[c]
        return remote(upd.at[span(0, c)], inbox.at[slot, pl.ds(start, count)],
                      rs_send.at[0, c], rs_recv.at[slot, c], owner(slot // 2), 1)

    def ag_copy(d, c):
        own = res.at[span(0, c)]
        return remote(own, own, ag_send.at[d, c], ag_recv.at[(chips - d) % chips, c], owner(d), 1)

    def fw_copy(d, c):
        part = res.at[span(d, c)]
        return remote(part, part, fw_send.at[d, c], ag_recv.at[d, c], chip, 0)

    def ag_arrival(d, c):
        part = res.at[span(d, c)]
        return remote(part, part, fw_send.at[d, c], ag_recv.at[d, c], chip, 0)

    def x_pair(b):
        start = pl.multiple_of(b * (2 * width), 2 * width)
        return x[pl.ds(start, width)], x[pl.ds(start + width, width)]

    def two_by_two(coef):
        zero = jnp.zeros_like(coef)
        top = jnp.concatenate([coef, zero], axis=1)
        low = jnp.concatenate([zero, coef], axis=1)
        return jnp.concatenate([top, low], axis=0).astype(jnp.bfloat16)

    def block_product(lhs, b):
        return jnp.dot(lhs, xt[b], preferred_element_type=jnp.float32).astype(jnp.bfloat16)

    def gradient_term(resid, b):
        return jnp.dot(resid.astype(jnp.bfloat16), jnp.concatenate(x_pair(b), axis=1),
                       preferred_element_type=jnp.float32)

    def gradient_of(acc):
        return (acc[:8, :feats] + acc[8:, feats:]) * (1.0 / samples)

    def scatter(product, ready=None):
        def compute(c):
            if ready is not None:
                ready(c)
            return [[product(b) for b in blocks_of(d, c)] for d in everyone]

        values = compute(0)
        for c in range(len(chunks)):
            for d, parts in zip(everyone, values):
                for b, part in zip(blocks_of(d, c), parts):
                    upd[b] = part
            if c + 1 < len(chunks):
                values = compute(c + 1)
            for d in others:
                rs_copy(d, c).start()
            on_helper(lambda: rs_copy(0, c).start())

    def sum_and_gather(scale):
        def body():
            for c in range(len(chunks)):
                for slot in range(group):
                    if slot != 1:
                        rs_arrival(slot, c).wait_recv()
                start, count = chunks[c]
                for k in range(start, start + count):
                    b = chip * per_owner + k
                    total = upd[b].astype(jnp.float32)
                    for slot in range(group):
                        if slot != 1:
                            total = total + inbox[slot, k].astype(jnp.float32)
                    res[b] = res[b] - scale * total
                for d in others:
                    ag_copy(d, c).start()
                fw_copy(0, c).start()
        on_owner(body)

    def gather_arrivals(use):
        for c in range(len(chunks)):
            on_helper(lambda: ag_arrival(0, c).wait_recv())
            for d in others[::-1]:
                ag_arrival(d, c).wait_recv()
                on_owner(lambda: fw_copy(d, c).start())
            use([b for d in everyone for b in blocks_of(d, c)])

    def wait_sends():
        for c in range(len(chunks)):
            for d in others:
                rs_copy(d, c).wait_send()

        def helper():
            for c in range(len(chunks)):
                rs_copy(0, c).wait_send()

        def owning():
            for c in range(len(chunks)):
                for d in others:
                    ag_copy(d, c).wait_send()
                for d in everyone:
                    fw_copy(d, c).wait_send()

        on_helper(helper)
        on_owner(owning)

    w_copy = pltpu.make_async_copy(w_hbm, w_in, w_sem)
    w_copy.start()
    for c in range(len(chunks)):
        for d in everyone:
            x_copy(d, c).start()

    def load_targets():
        for k in range(per_owner):
            for h in (0, 1):
                y_copy(k, h).start()
        for k in range(per_owner):
            for h in (0, 1):
                y_copy(k, h).wait()

    barrier = pltpu.get_barrier_semaphore()
    for step in range(1, group):
        pl.semaphore_signal(barrier, inc=1, device_id={"feat": (me + step) % group}, device_id_type=MESH)
    w_copy.wait()
    weights = w_in[...]
    start_lhs = two_by_two(weights)
    pl.semaphore_wait(barrier, group - 1)

    def first_product(b):
        rows = jnp.concatenate(x_pair(b), axis=1)
        full = lax.dot_general(start_lhs, rows, (((1,), (1,)), ((), ())), preferred_element_type=jnp.float32)
        return full.astype(jnp.bfloat16)

    def x_ready(c):
        for d in everyone:
            x_copy(d, c).wait()

    scatter(first_product, x_ready)
    on_owner(load_targets)

    def prepare(b, total):
        first, second = x_pair(b)
        xt[b, :feats] = first.T
        xt[b, feats:] = second.T
        for part in (first.astype(jnp.float32), second.astype(jnp.float32)):
            total = total + jnp.sum((part * part).reshape(width // 8, 8, feats), axis=0)
        return total

    squares = jnp.zeros((8, feats), jnp.float32)
    squares = lax.fori_loop(0, blocks // 2, prepare, squares)
    sum_and_gather(1.0)
    squares = lax.fori_loop(blocks // 2, blocks, prepare, squares)
    step_size = samples / (group * jnp.sum(squares))

    def sweep(sweep_idx, weights):
        acc = [jnp.zeros((16, 2 * feats), jnp.float32)]

        def use(parts):
            for b in parts:
                acc[0] = acc[0] + gradient_term(res[b], b)

        gather_arrivals(use)
        coef = step_size * (gradient_of(acc[0]) - RIDGE * weights)
        for step_idx in range(1, LOCAL_STEPS):
            lhs = two_by_two(coef)
            total = jnp.zeros((16, 2 * feats), jnp.float32)
            queue = [block_product(lhs, b) for b in range(AHEAD)]
            for b in range(blocks):
                if b + AHEAD < blocks:
                    queue.append(block_product(lhs, b + AHEAD))
                product = queue.pop(0).astype(jnp.float32)
                total = total + gradient_term(res[b] - group * product, b)
            coef = coef + step_size * (gradient_of(total) - RIDGE * (weights + coef))
        lhs = two_by_two(coef)
        wait_sends()
        scatter(lambda b: block_product(lhs, b))
        sum_and_gather(GAMMA)
        return weights + GAMMA * coef

    w_out[...] = lax.fori_loop(0, SWEEPS, sweep, weights)

    def put(parts):
        for b in parts:
            for h in (0, 1):
                cols = pl.ds(pl.multiple_of((b * 2 + h) * width, width), width)
                r_out[:, cols] = res[b, 8 * h:8 * h + 8]

    gather_arrivals(put)
    wait_sends()


def solution(mesh):
    group = mesh.shape["feat"]

    def per_device(design, w_init, targets):
        samples, feats = design.shape
        outs = targets.shape[1]
        chips = group // 2
        per_owner = samples // (2 * LANES * chips)
        blocks = chips * per_owner
        parts = len(CHUNKS)
        hbm = pl.BlockSpec(memory_space=pltpu.HBM)
        vmem = pl.BlockSpec(memory_space=pltpu.VMEM)
        dma = pltpu.SemaphoreType.DMA
        weights, residual = pl.pallas_call(
            functools.partial(kernel, group, per_owner),
            out_shape=(jax.ShapeDtypeStruct((outs, feats), jnp.float32),
                       jax.ShapeDtypeStruct((outs, samples), jnp.float32)),
            in_specs=[hbm, hbm, hbm],
            out_specs=(vmem, vmem),
            scratch_shapes=[
                pltpu.VMEM((samples, feats), jnp.bfloat16),
                pltpu.VMEM((blocks, 2 * feats, LANES), jnp.bfloat16),
                pltpu.VMEM((outs, feats), jnp.float32),
                pltpu.VMEM((blocks, 2 * outs, LANES), jnp.float32),
                pltpu.VMEM((blocks, 2 * outs, LANES), jnp.bfloat16),
                pltpu.VMEM((group, per_owner, 2 * outs, LANES), jnp.bfloat16),
                dma((chips, parts)),
                dma,
                dma((2 * per_owner,)),
                dma((chips, parts)),
                dma((group, parts)),
                dma((chips, parts)),
                dma((chips, parts)),
                dma((chips, parts)),
            ],
            compiler_params=pltpu.CompilerParams(collective_id=0, has_side_effects=True,
                                                 vmem_limit_bytes=67043328),
        )(design, w_init.T, targets.T)
        return weights.T, residual.T

    return jax.shard_map(
        per_device,
        mesh=mesh,
        in_specs=(P(None, ("prob", "feat")), P(("prob", "feat"), None), P("prob", None)),
        out_specs=(P(("prob", "feat"), None), P("prob", None)),
        check_vma=False,
    )
```

time: 481 us -> 91.9 us (0.19)
  waiting for transfers between devices: 375 us -> 0 us
  Pallas kernels: 0 us -> 87.8 us
  matrix products: 78.8 us -> 0 us
  between operations: 14.9 us -> 0.64 us
  other arithmetic: 9.59 us -> 0 us
    psum x7 -> x0, waiting for transfers between devices: 375 us -> none  [the longest x6 323 us: per_device(): residual = residual - GAMMA * lax.psum(update, 'feat')]
    pallas_call x0 -> x1, Pallas kernels: none -> 87.8 us  [per_device(): pl.pallas_call(functools.partial(kernel, group, per_owner), out_shape=(ja...]
    dot_general x19 -> x0, matrix products: 78.8 us -> none  [the longest x12 49.5 us: left_product(): lax.dot_general(x_block, resid_part.astype(jnp.bfloat16), (((0,), (0,)),...]
    sub x4 -> x0, other arithmetic: 5.22 us -> none  [the longest x3 4.13 us: per_device(): residual = residual - GAMMA * lax.psum(update, 'feat')]
  transfers between devices with their start and end apart: 7 -> 0, of which waited for: 7 -> 0; matrix products, arithmetic and copies ran while one was open for 1% -> 0% of each run, Pallas kernels for 0% -> 0%
where the time goes in v2:
time: 91.9 us; the launch traced here: 91.6 us
  Pallas kernels  87.8 us (96%)
  local copies, waits for them, and re-layouts  3.13 us (3%)
    pallas_call x1, Pallas kernels, per_device(): pl.pallas_call(functools.partial(kernel, group, per_owner), out_shape=(ja...  87.8 us
    unnamed x2, local copies, waits for them, and re-layouts  3.13 us

profile of v2, /device:TPU:81, one launch (start us, length us, event | category | flops | bytes accessed | tf_op | source)
XLA Modules:
  0.0 91.6 jit_solution(1191681979552460540)
XLA Ops:
  0.6 87.8 %shard_map.50 = (f32[8,128]{1,0:T(8,128)}, f32[8,16384]{1,0:T(8,128)}) custom-call(bf16[16384,128]{1,0:T(8,128)(2,1)} %x_hbm.1, f32[8,128]{1,0:T(8,128)} %bitcast.7, f32[8,16384]{1,0:T(8,128)} %bitcast.5), custom_call_target="tpu_custom_call" | custom-call | tf_op jit(solution)/shard_map/pallas_call | solution.py:273
  88.4 1.3 %copy.7 = f32[128,8]{0,1:T(8,128)} copy(f32[128,8]{0,1:T(8,128)} %bitcast.6) | data formatting | bytes 8192
  89.7 1.9 %copy.8 = f32[16384,8]{0,1:T(8,128)} copy(f32[16384,8]{0,1:T(8,128)} %bitcast.4) | data formatting | bytes 1048576

commit v3 on v2

v3 whole, which is shorter than its diff:
```python
import functools

import jax
import jax.numpy as jnp
from jax import lax
from jax.experimental import pallas as pl
from jax.experimental.pallas import tpu as pltpu
from jax.sharding import PartitionSpec as P

LOCAL_STEPS = 2
SWEEPS = 6
RIDGE = 0.01
GAMMA = 0.75

LANES = 256
PARTS = 4
CHUNKS = (2, 2)
AHEAD = 1
MESH = pl.DeviceIdType.MESH


def kernel(group, per_owner, x_hbm, w_in, y_hbm, w_out, r_out,
           x, xt, y_in, res, upd, inbox,
           x_sem, y_sem, rs_send, rs_recv, ag_send, ag_recv, fw_send):
    chips = group // 2
    width = LANES
    blocks = chips * per_owner
    samples, feats = x.shape
    rows = w_in.shape[0] // 2
    size = PARTS * width
    halves = (0, 1)
    me = lax.axis_index("feat")
    chip, core = me // 2, me % 2

    others = sorted(range(1, chips), key=lambda d: -min(d, chips - d))
    everyone = others + [0]
    chunks = []
    for count in CHUNKS:
        chunks.append((sum(n for _, n in chunks), count))
    assert sum(CHUNKS) == per_owner

    def owner(d):
        return (chip + d) % chips

    def on_owner(body):
        pl.when(core == 1)(body)

    def on_helper(body):
        pl.when(core == 0)(body)

    def span(d, c):
        start, count = chunks[c]
        return pl.ds(owner(d) * per_owner + start, count)

    def blocks_of(d, c):
        start, count = chunks[c]
        return [owner(d) * per_owner + start + k for k in range(count)]

    def x_copy(d, c):
        start, count = chunks[c]
        part = pl.ds(pl.multiple_of((owner(d) * per_owner + start) * size, size), count * size)
        return pltpu.make_async_copy(x_hbm.at[part], x.at[part], x_sem.at[d, c])

    def y_copy():
        cols = pl.ds(pl.multiple_of(chip * (per_owner * size), per_owner * size), per_owner * size)
        return pltpu.make_async_copy(y_hbm.at[:, cols], y_in, y_sem)

    def remote(src, dst, send, recv, chip_to, core_to):
        return pltpu.make_async_remote_copy(src_ref=src, dst_ref=dst, send_sem=send, recv_sem=recv,
                                            device_id={"feat": chip_to * 2 + core_to}, device_id_type=MESH)

    def rs_copy(p, d, c):
        slot = (chips - d) % chips * 2 + core
        start, count = chunks[c]
        return remote(upd.at[p, span(d, c)], inbox.at[p, slot, pl.ds(start, count)],
                      rs_send.at[p, d, c], rs_recv.at[p, slot, c], owner(d), 1)

    def rs_arrival(p, slot, c):
        start, count = chunks[c]
        return remote(upd.at[p, span(0, c)], inbox.at[p, slot, pl.ds(start, count)],
                      rs_send.at[p, 0, c], rs_recv.at[p, slot, c], owner(slot // 2), 1)

    def ag_copy(p, d, c):
        own = res.at[p, span(0, c)]
        return remote(own, own, ag_send.at[p, d, c], ag_recv.at[p, (chips - d) % chips, c], owner(d), 1)

    def fw_copy(p, d, c):
        part = res.at[p, span(d, c)]
        return remote(part, part, fw_send.at[p, d, c], ag_recv.at[p, d, c], chip, 0)

    def x_parts(b):
        start = pl.multiple_of(b * size, size)
        return [x[pl.ds(start + q * width, width)] for q in range(PARTS)]

    def diagonal(coef):
        tall = jnp.concatenate([coef] * PARTS, axis=0)
        place = lax.broadcasted_iota(jnp.int32, tall.shape, 0) // rows
        return jnp.concatenate([jnp.where(place == q, tall, 0.0) for q in range(PARTS)], axis=1).astype(jnp.bfloat16)

    def block_product(lhs, b):
        return jnp.dot(lhs, xt[b], preferred_element_type=jnp.float32).astype(jnp.bfloat16)

    def gradient_term(resid, b):
        return jnp.dot(resid.astype(jnp.bfloat16), jnp.concatenate(x_parts(b), axis=1),
                       preferred_element_type=jnp.float32)

    def gradient_of(acc):
        total = acc[:rows, :feats]
        for q in range(1, PARTS):
            total = total + acc[q * rows:(q + 1) * rows, q * feats:(q + 1) * feats]
        return total * (1.0 / samples)

    def send_chunk(p, c):
        for d in others:
            rs_copy(p, d, c).start()
        on_helper(lambda: rs_copy(p, 0, c).start())

    def scatter(p, lhs):
        for c in range(len(chunks)):
            values = [(b, block_product(lhs, b)) for d in everyone for b in blocks_of(d, c)]
            for b, value in values:
                upd[p, b] = value
            send_chunk(p, c)

    def sum_and_gather(p, scale):
        def body():
            for c in range(len(chunks)):
                for slot in range(group):
                    if slot != 1:
                        rs_arrival(p, slot, c).wait_recv()
                start, count = chunks[c]
                for k in range(start, start + count):
                    b = chip * per_owner + k
                    total = upd[p, b].astype(jnp.float32)
                    for slot in range(group):
                        if slot != 1:
                            total = total + inbox[p, slot, k].astype(jnp.float32)
                    res[p, b] = res[p, b] - scale * total
                for d in others:
                    ag_copy(p, d, c).start()
                fw_copy(p, 0, c).start()
        on_owner(body)

    def gather_arrivals(p, use, early=False):
        for c in range(len(chunks)):
            if early and c == len(chunks) - 1:
                wait_scatter(p)
            on_helper(lambda: fw_copy(p, 0, c).wait_recv())
            for d in others[::-1]:
                fw_copy(p, d, c).wait_recv()
                on_owner(lambda: fw_copy(p, d, c).start())
            use([b for d in everyone for b in blocks_of(d, c)])

    def wait_scatter(p):
        for c in range(len(chunks)):
            for d in others:
                rs_copy(p, d, c).wait_send()

        def helper():
            for c in range(len(chunks)):
                rs_copy(p, 0, c).wait_send()

        on_helper(helper)

    def wait_gather(p):
        def owning():
            for c in range(len(chunks)):
                for d in others:
                    ag_copy(p, d, c).wait_send()
                for d in everyone:
                    fw_copy(p, d, c).wait_send()
        on_owner(owning)

    for c in range(len(chunks)):
        for d in everyone:
            x_copy(d, c).start()
    on_owner(lambda: y_copy().start())

    barrier = pltpu.get_barrier_semaphore()
    for step in range(1, group):
        pl.semaphore_signal(barrier, inc=1, device_id={"feat": (me + step) % group}, device_id_type=MESH)
    start_weights = tuple(w_in[p * rows:(p + 1) * rows] for p in halves)
    start_lhs = jnp.concatenate([diagonal(start_weights[p]) for p in halves], axis=0)

    for c in range(len(chunks)):
        for d in everyone:
            x_copy(d, c).wait()
        for b in [b for d in everyone for b in blocks_of(d, c)]:
            both = lax.dot_general(start_lhs, jnp.concatenate(x_parts(b), axis=1), (((1,), (1,)), ((), ())),
                                   preferred_element_type=jnp.float32).astype(jnp.bfloat16)
            for p in halves:
                upd[p, b] = both[p * PARTS * rows:(p + 1) * PARTS * rows]
        if c == 0:
            pl.semaphore_wait(barrier, group - 1)
        send_chunk(0, c)
    for c in range(len(chunks)):
        send_chunk(1, c)

    def prepare(b, total):
        for q, part in enumerate(x_parts(b)):
            xt[b, q * feats:(q + 1) * feats] = part.T
            wide = part.astype(jnp.float32)
            total = total + jnp.sum((wide * wide).reshape(width // 8, 8, feats), axis=0)
        return total

    squares = jnp.zeros((8, feats), jnp.float32)
    squares = lax.fori_loop(0, blocks // 2, prepare, squares)

    def take_targets():
        y_copy().wait()
        for p in halves:
            for k in range(per_owner):
                res[p, chip * per_owner + k] = jnp.concatenate(
                    [y_in[p * rows:(p + 1) * rows, (k * PARTS + q) * width:(k * PARTS + q + 1) * width]
                     for q in range(PARTS)], axis=0)

    on_owner(take_targets)
    for p in halves:
        sum_and_gather(p, 1.0)
    squares = lax.fori_loop(blocks // 2, blocks, prepare, squares)
    step_size = samples / (group * jnp.sum(squares))

    def half_sweep(p, weights):
        acc = [jnp.zeros((PARTS * rows, PARTS * feats), jnp.float32)]

        def use(parts):
            for b in parts:
                acc[0] = acc[0] + gradient_term(res[p, b], b)

        gather_arrivals(p, use, True)
        coef = step_size * (gradient_of(acc[0]) - RIDGE * weights)
        for step_idx in range(1, LOCAL_STEPS):
            lhs = diagonal(coef)
            total = jnp.zeros((PARTS * rows, PARTS * feats), jnp.float32)
            queue = [block_product(lhs, b) for b in range(AHEAD)]
            for b in range(blocks):
                if b + AHEAD < blocks:
                    queue.append(block_product(lhs, b + AHEAD))
                product = queue.pop(0).astype(jnp.float32)
                total = total + gradient_term(res[p, b] - group * product, b)
            coef = coef + step_size * (gradient_of(total) - RIDGE * (weights + coef))
        wait_gather(p)
        scatter(p, diagonal(coef))
        return weights + GAMMA * coef

    def sweep(sweep_idx, weights):
        weights = tuple(half_sweep(p, weights[p]) for p in halves)
        for p in halves:
            sum_and_gather(p, GAMMA)
        return weights

    end_weights = lax.fori_loop(0, SWEEPS, sweep, start_weights)
    for p in halves:
        w_out[p * rows:(p + 1) * rows] = end_weights[p]

        def put(parts):
            for b in parts:
                for q in range(PARTS):
                    cols = pl.ds(pl.multiple_of((b * PARTS + q) * width, width), width)
                    r_out[p * rows:(p + 1) * rows, cols] = res[p, b, q * rows:(q + 1) * rows]

        gather_arrivals(p, put)
        wait_scatter(p)
        wait_gather(p)


def solution(mesh):
    group = mesh.shape["feat"]

    def per_device(design, w_init, targets):
        samples, feats = design.shape
        outs = targets.shape[1]
        chips = group // 2
        blocks = samples // (PARTS * LANES)
        per_owner = blocks // chips
        parts = len(CHUNKS)
        rows = PARTS * outs // 2
        hbm = pl.BlockSpec(memory_space=pltpu.HBM)
        vmem = pl.BlockSpec(memory_space=pltpu.VMEM)
        dma = pltpu.SemaphoreType.DMA
        weights, residual = pl.pallas_call(
            functools.partial(kernel, group, per_owner),
            out_shape=(jax.ShapeDtypeStruct((outs, feats), jnp.float32),
                       jax.ShapeDtypeStruct((outs, samples), jnp.float32)),
            in_specs=[hbm, vmem, hbm],
            out_specs=(vmem, vmem),
            scratch_shapes=[
                pltpu.VMEM((samples, feats), jnp.bfloat16),
                pltpu.VMEM((blocks, PARTS * feats, LANES), jnp.bfloat16),
                pltpu.VMEM((outs, per_owner * PARTS * LANES), jnp.float32),
                pltpu.VMEM((2, blocks, rows, LANES), jnp.float32),
                pltpu.VMEM((2, blocks, rows, LANES), jnp.bfloat16),
                pltpu.VMEM((2, group, per_owner, rows, LANES), jnp.bfloat16),
                dma((chips, parts)),
                dma,
                dma((2, chips, parts)),
                dma((2, group, parts)),
                dma((2, chips, parts)),
                dma((2, chips, parts)),
                dma((2, chips, parts)),
            ],
            compiler_params=pltpu.CompilerParams(collective_id=0, has_side_effects=True,
                                                 vmem_limit_bytes=56000000),
        )(design, w_init.T, targets.T)
        return weights.T, residual.T

    return jax.shard_map(
        per_device,
        mesh=mesh,
        in_specs=(P(None, ("prob", "feat")), P(("prob", "feat"), None), P("prob", None)),
        out_specs=(P(("prob", "feat"), None), P("prob", None)),
        check_vma=False,
    )
```

time: 91.9 us -> 84 us (0.914)
  Pallas kernels: 87.8 us -> 81.2 us
  local copies, waits for them, and re-layouts: 3.13 us -> 2.07 us
    pallas_call x1, Pallas kernels: 87.8 us -> 81.2 us  [per_device(): pl.pallas_call(functools.partial(kernel, group, per_owner), out_shape=(ja...]
    unnamed x2 -> x4, local copies, waits for them, and re-layouts: 3.13 us -> 2.07 us
where the time goes in v3:
time: 84 us; the launch traced here: 83.9 us
  Pallas kernels  81.2 us (97%)
  local copies, waits for them, and re-layouts  2.07 us (2%)
    pallas_call x1, Pallas kernels, per_device(): pl.pallas_call(functools.partial(kernel, group, per_owner), out_shape=(ja...  81.2 us
    unnamed x4, local copies, waits for them, and re-layouts  2.07 us

profile of v3, /device:TPU:81, one launch (start us, length us, event | category | flops | bytes accessed | tf_op | source)
XLA Modules:
  0.0 83.9 jit_solution(5958342616159648958)
XLA Ops:
  0.6 0.0 copy-start
  0.6 0.7 copy-done
  1.3 81.2 %shard_map.50 = (f32[8,128]{1,0:T(8,128)S(1)}, f32[8,16384]{1,0:T(8,128)S(1)}) custom-call(bf16[16384,128]{1,0:T(8,128)(2,1)} %x_hbm.1, f32[8,128]{1,0:T(8,128)S(1)} %bitcast.6, f32[8,16384]{1,0:T(8,128)} %bitcast.7), custom_call_target="tpu_custom_call" | custom-call | tf_op jit(solution)/shard_map/pallas_call | solution.py:281
  82.5 0.6 copy.7
  83.1 0.8 copy.8
Async XLA Ops:
  0.6 0.7 copy-start

commit v4 on v3

--- a/solution.py
+++ b/solution.py
@@ -15,7 +15,7 @@
 LANES = 256
 PARTS = 4
 CHUNKS = (2, 2)
-AHEAD = 1
+AHEAD = 4
 MESH = pl.DeviceIdType.MESH
 
 

time: 84 us -> 82.9 us (0.987)
  Pallas kernels: 81.2 us -> 80 us
    pallas_call x1, Pallas kernels: 81.2 us -> 80 us  [per_device(): pl.pallas_call(functools.partial(kernel, group, per_owner), out_shape=(ja...]
where the time goes in v4:
time: 82.9 us; the launch traced here: 82.8 us
  Pallas kernels  80 us (97%)
  local copies, waits for them, and re-layouts  2.07 us (2%)
    pallas_call x1, Pallas kernels, per_device(): pl.pallas_call(functools.partial(kernel, group, per_owner), out_shape=(ja...  80 us
    unnamed x4, local copies, waits for them, and re-layouts  2.07 us

profile of v4, /device:TPU:81, one launch (start us, length us, event | category | flops | bytes accessed | tf_op | source)
XLA Modules:
  0.0 82.8 jit_solution(7994947757969473848)
XLA Ops:
  0.6 0.0 copy-start
  0.6 0.7 copy-done
  1.3 80.0 %shard_map.50 = (f32[8,128]{1,0:T(8,128)S(1)}, f32[8,16384]{1,0:T(8,128)S(1)}) custom-call(bf16[16384,128]{1,0:T(8,128)(2,1)} %x_hbm.1, f32[8,128]{1,0:T(8,128)S(1)} %bitcast.6, f32[8,16384]{1,0:T(8,128)} %bitcast.7), custom_call_target="tpu_custom_call" | custom-call | tf_op jit(solution)/shard_map/pallas_call | solution.py:281
  81.4 0.6 copy.7
  82.0 0.8 copy.8
Async XLA Ops:
  0.6 0.7 copy-start

commit v5 on v4

--- a/solution.py
+++ b/solution.py
@@ -19,8 +19,8 @@
 MESH = pl.DeviceIdType.MESH
 
 
-def kernel(group, per_owner, x_hbm, w_in, y_hbm, w_out, r_out,
-           x, xt, y_in, res, upd, inbox,
+def kernel(group, per_owner, x_hbm, w_hbm, y_hbm, w_out, r_out,
+           x, xt, w_in, w_sem, y_in, res, upd, inbox,
            x_sem, y_sem, rs_send, rs_recv, ag_send, ag_recv, fw_send):
     chips = group // 2
     width = LANES
@@ -70,15 +70,13 @@
                                             device_id={"feat": chip_to * 2 + core_to}, device_id_type=MESH)
 
     def rs_copy(p, d, c):
-        slot = (chips - d) % chips * 2 + core
+        slot = ((chips - d) % chips * 2 + 1 - core + group - 1) % group
         start, count = chunks[c]
-        return remote(upd.at[p, span(d, c)], inbox.at[p, slot, pl.ds(start, count)],
-                      rs_send.at[p, d, c], rs_recv.at[p, slot, c], owner(d), 1)
-
-    def rs_arrival(p, slot, c):
-        start, count = chunks[c]
-        return remote(upd.at[p, span(0, c)], inbox.at[p, slot, pl.ds(start, count)],
-                      rs_send.at[p, 0, c], rs_recv.at[p, slot, c], owner(slot // 2), 1)
+        return remote(upd.at[p, span(d, c)], inbox.at[p, c, slot],
+                      rs_send.at[p, d, c], rs_recv.at[p, c], owner(d), 1)
+
+    def rs_arrivals(p, c):
+        return remote(inbox.at[p, c], inbox.at[p, c], rs_send.at[p, 0, c], rs_recv.at[p, c], chip, 0)
 
     def ag_copy(p, d, c):
         own = res.at[p, span(0, c)]
@@ -125,16 +123,13 @@
     def sum_and_gather(p, scale):
         def body():
             for c in range(len(chunks)):
-                for slot in range(group):
-                    if slot != 1:
-                        rs_arrival(p, slot, c).wait_recv()
+                rs_arrivals(p, c).wait_recv()
                 start, count = chunks[c]
                 for k in range(start, start + count):
                     b = chip * per_owner + k
                     total = upd[p, b].astype(jnp.float32)
-                    for slot in range(group):
-                        if slot != 1:
-                            total = total + inbox[p, slot, k].astype(jnp.float32)
+                    for slot in range(group - 1):
+                        total = total + inbox[p, c, slot, k - start].astype(jnp.float32)
                     res[p, b] = res[p, b] - scale * total
                 for d in others:
                     ag_copy(p, d, c).start()
@@ -145,10 +140,17 @@
         for c in range(len(chunks)):
             if early and c == len(chunks) - 1:
                 wait_scatter(p)
-            on_helper(lambda: fw_copy(p, 0, c).wait_recv())
-            for d in others[::-1]:
-                fw_copy(p, d, c).wait_recv()
-                on_owner(lambda: fw_copy(p, d, c).start())
+            def owning():
+                for d in others[::-1]:
+                    fw_copy(p, d, c).wait_recv()
+                    fw_copy(p, d, c).start()
+
+            def helper():
+                for d in everyone[::-1]:
+                    fw_copy(p, d, c).wait_recv()
+
+            on_owner(owning)
+            on_helper(helper)
             use([b for d in everyone for b in blocks_of(d, c)])
 
     def wait_scatter(p):
@@ -171,6 +173,8 @@
                     fw_copy(p, d, c).wait_send()
         on_owner(owning)
 
+    w_copy = pltpu.make_async_copy(w_hbm, w_in, w_sem)
+    w_copy.start()
     for c in range(len(chunks)):
         for d in everyone:
             x_copy(d, c).start()
@@ -179,6 +183,7 @@
     barrier = pltpu.get_barrier_semaphore()
     for step in range(1, group):
         pl.semaphore_signal(barrier, inc=1, device_id={"feat": (me + step) % group}, device_id_type=MESH)
+    w_copy.wait()
     start_weights = tuple(w_in[p * rows:(p + 1) * rows] for p in halves)
     start_lhs = jnp.concatenate([diagonal(start_weights[p]) for p in halves], axis=0)
 
@@ -282,26 +287,28 @@
             functools.partial(kernel, group, per_owner),
             out_shape=(jax.ShapeDtypeStruct((outs, feats), jnp.float32),
                        jax.ShapeDtypeStruct((outs, samples), jnp.float32)),
-            in_specs=[hbm, vmem, hbm],
+            in_specs=[hbm, hbm, hbm],
             out_specs=(vmem, vmem),
             scratch_shapes=[
                 pltpu.VMEM((samples, feats), jnp.bfloat16),
                 pltpu.VMEM((blocks, PARTS * feats, LANES), jnp.bfloat16),
+                pltpu.VMEM((outs, feats), jnp.float32),
+                dma,
                 pltpu.VMEM((outs, per_owner * PARTS * LANES), jnp.float32),
                 pltpu.VMEM((2, blocks, rows, LANES), jnp.float32),
                 pltpu.VMEM((2, blocks, rows, LANES), jnp.bfloat16),
-                pltpu.VMEM((2, group, per_owner, rows, LANES), jnp.bfloat16),
+                pltpu.VMEM((2, parts, group - 1, per_owner // parts, rows, LANES), jnp.bfloat16),
                 dma((chips, parts)),
                 dma,
                 dma((2, chips, parts)),
-                dma((2, group, parts)),
+                dma((2, parts)),
                 dma((2, chips, parts)),
                 dma((2, chips, parts)),
                 dma((2, chips, parts)),
             ],
             compiler_params=pltpu.CompilerParams(collective_id=0, has_side_effects=True,
                                                  vmem_limit_bytes=56000000),
-        )(design, w_init.T, targets.T)
+        )(design, pltpu.with_memory_space_constraint(w_init.T, pltpu.HBM), targets.T)
         return weights.T, residual.T
 
     return jax.shard_map(

time: 82.9 us -> 82 us (0.989)
    unnamed x4 -> x2, local copies, waits for them, and re-layouts: 2.07 us -> 1.39 us
where the time goes in v5:
time: 82 us; the launch traced here: 81.8 us
  Pallas kernels  79.8 us (97%)
  local copies, waits for them, and re-layouts  1.39 us (2%)
    pallas_call x1, Pallas kernels, per_device(): pl.pallas_call(functools.partial(kernel, group, per_owner), out_shape=(ja...  79.8 us

profile of v5, /device:TPU:81, one launch (start us, length us, event | category | flops | bytes accessed | tf_op | source)
XLA Modules:
  0.0 81.8 jit_solution(5555832515887842327)
XLA Ops:
  0.6 79.8 %shard_map.50 = (f32[8,128]{1,0:T(8,128)S(1)}, f32[8,16384]{1,0:T(8,128)S(1)}) custom-call(bf16[16384,128]{1,0:T(8,128)(2,1)} %x_hbm.1, f32[8,128]{1,0:T(8,128)} %bitcast.7, f32[8,16384]{1,0:T(8,128)} %bitcast.6), custom_call_target="tpu_custom_call" | custom-call | tf_op jit(solution)/shard_map/pallas_call | solution.py:286
  80.5 0.6 copy.7
  81.1 0.8 copy.8

commit v6 on v5

--- a/solution.py
+++ b/solution.py
@@ -114,11 +114,22 @@
         on_helper(lambda: rs_copy(p, 0, c).start())
 
     def scatter(p, lhs):
+        last = len(chunks) - 1
         for c in range(len(chunks)):
-            values = [(b, block_product(lhs, b)) for d in everyone for b in blocks_of(d, c)]
+            ds = others if c < last else everyone
+            values = [(b, block_product(lhs, b)) for d in ds for b in blocks_of(d, c)]
+            if c == last:
+                values += [(b, block_product(lhs, b)) for k in range(last) for b in blocks_of(0, k)]
             for b, value in values:
                 upd[p, b] = value
-            send_chunk(p, c)
+            for d in others:
+                rs_copy(p, d, c).start()
+
+        def to_owner():
+            for c in range(len(chunks)):
+                rs_copy(p, 0, c).start()
+
+        on_helper(to_owner)
 
     def sum_and_gather(p, scale):
         def body():

time: 82 us -> 81.5 us (level)
  no operation moved by 1% of the time
where the time goes in v6:
time: 81.5 us; the launch traced here: 81.4 us
  Pallas kernels  79.4 us (97%)
  local copies, waits for them, and re-layouts  1.39 us (2%)
    pallas_call x1, Pallas kernels, per_device(): pl.pallas_call(functools.partial(kernel, group, per_owner), out_shape=(ja...  79.4 us

profile of v6, /device:TPU:81, one launch (start us, length us, event | category | flops | bytes accessed | tf_op | source)
XLA Modules:
  0.0 81.4 jit_solution(16410262878573060506)
XLA Ops:
  0.6 79.4 %shard_map.50 = (f32[8,128]{1,0:T(8,128)S(1)}, f32[8,16384]{1,0:T(8,128)S(1)}) custom-call(bf16[16384,128]{1,0:T(8,128)(2,1)} %x_hbm.1, f32[8,128]{1,0:T(8,128)} %bitcast.7, f32[8,16384]{1,0:T(8,128)} %bitcast.6), custom_call_target="tpu_custom_call" | custom-call | tf_op jit(solution)/shard_map/pallas_call | solution.py:297
  80.0 0.6 copy.7
  80.6 0.8 copy.8

commit v7 on v6

--- a/solution.py
+++ b/solution.py
@@ -157,12 +157,15 @@
                     fw_copy(p, d, c).start()
 
             def helper():
-                for d in everyone[::-1]:
+                for k in range(len(chunks) if c == 0 else 0):
+                    fw_copy(p, 0, k).wait_recv()
+                for d in others[::-1]:
                     fw_copy(p, d, c).wait_recv()
 
             on_owner(owning)
             on_helper(helper)
-            use([b for d in everyone for b in blocks_of(d, c)])
+            own = [b for k in range(len(chunks)) for b in blocks_of(0, k)] if c == 0 else []
+            use([b for d in others for b in blocks_of(d, c)] + own)
 
     def wait_scatter(p):
         for c in range(len(chunks)):

time: 81.5 us -> 81.3 us (level)
  no operation moved by 1% of the time
where the time goes in v7:
time: 81.3 us; the launch traced here: 81.2 us
  Pallas kernels  79.2 us (97%)
  local copies, waits for them, and re-layouts  1.39 us (2%)
    pallas_call x1, Pallas kernels, per_device(): pl.pallas_call(functools.partial(kernel, group, per_owner), out_shape=(ja...  79.2 us

profile of v7, /device:TPU:81, one launch (start us, length us, event | category | flops | bytes accessed | tf_op | source)
XLA Modules:
  0.0 81.2 jit_solution(16255249259777139356)
XLA Ops:
  0.6 79.2 %shard_map.50 = (f32[8,128]{1,0:T(8,128)S(1)}, f32[8,16384]{1,0:T(8,128)S(1)}) custom-call(bf16[16384,128]{1,0:T(8,128)(2,1)} %x_hbm.1, f32[8,128]{1,0:T(8,128)} %bitcast.7, f32[8,16384]{1,0:T(8,128)} %bitcast.6), custom_call_target="tpu_custom_call" | custom-call | tf_op jit(solution)/shard_map/pallas_call | solution.py:300
  79.8 0.6 copy.7
  80.4 0.8 copy.8
